TPU v7x, 32 devices: a whole 2x2x4 slice. The times are simulated.
32 devices in a mesh: row: 8 (over z, y), col: 4 (over x, core).
Axes of the slice: x: 2, y: 2, z: 4, core: 2. Of those that a mesh axis runs over, the one named last changes fastest.
Arguments:
- new_dosage: float32 [4096, 1024], P(('col', 'row')), may hold values from 0 to 2
- old_dosage: float32 [16384, 1024], P(('row', 'col')), may hold values from 0 to 2
- grm: bfloat16 [16384, 4096], P('row', 'col'), may hold values from -1.5 to 1.5
- counts: int32 [8], P('col'), may hold values from 256 to 512
- affected: int32 [32, 8], P('row', 'col'), may hold values from 0 to 1, as said below
Outputs:
- updated: bfloat16 [16384, 4096], P('row', 'col')
Inputs may be any that keep to these rules, and one draw needn't show every extreme that they name: `affected`: the density of marked tile pairs differs from one tile of new samples to the next.
All inputs are finite; a program needn't handle non-finite values.
Results may differ from a plain program's by a relative error of at most 0.00115.
Values may be sent and summed in bfloat16 or wider, within the bound.
A program may use at most 128 MiB of HBM per device.

v0:
```python
import jax
import jax.numpy as jnp
from jax import lax
from jax.sharding import PartitionSpec as P

TILE = 512


def on_device(new_dosage, old_dosage, grm, counts, affected):
    devices = lax.axis_size("row") * lax.axis_size("col")
    totals = lax.psum(jnp.sum(old_dosage, axis=0), ("row", "col"))
    doubled = totals / (old_dosage.shape[0] * devices)
    spread = jnp.sqrt(doubled * (1.0 - 0.5 * doubled) + 0.1)
    usable = (jnp.arange(TILE)[None, :] < counts[:, None]).reshape(-1).astype(jnp.float32)
    snp_count = new_dosage.shape[1]
    contract = (((1,), (1,)), ((), ()))
    local_rows = new_dosage.shape[0]
    usable_mine = lax.dynamic_slice_in_dim(usable, lax.axis_index("row") * local_rows, local_rows)
    scores_mine = ((new_dosage - doubled) / spread * usable_mine[:, None]).astype(jnp.bfloat16)
    new_scores = lax.all_gather(scores_mine, "row", axis=0, tiled=True)
    old_mine = ((old_dosage - doubled) / spread).astype(jnp.bfloat16)
    product = lax.dot_general(
        lax.all_gather(old_mine, "col", axis=0, tiled=True),
        new_scores,
        contract,
        preferred_element_type=jnp.float32,
    )
    row_count, col_count = product.shape
    scaled = (product / snp_count).reshape(row_count // TILE, TILE, col_count // TILE, TILE)
    masked_update = scaled * affected.astype(jnp.float32)[:, None, :, None]
    return (grm.astype(jnp.float32) + masked_update.reshape(row_count, col_count)).astype(
        jnp.bfloat16
    )


def solution(mesh):
    in_specs = (
        P(("col", "row"), None),
        P(("row", "col"), None),
        P("row", "col"),
        P("col"),
        P("row", "col"),
    )
    out_specs = P("row", "col")
    return jax.shard_map(
        on_device, mesh=mesh, in_specs=in_specs, out_specs=out_specs, check_vma=False
    )
```

profile of v0, /device:TPU:1, one launch (start us, length us, event | category | flops | bytes accessed | tf_op | source)
XLA Modules:
  0.0 156.8 jit_solution(6402705490686522627)
XLA Ops:
  6.5 0.0 copy-start
  6.5 0.0 copy-start.1
  6.5 0.0 all-gather.5.cloned.1.call-start
  6.5 1.9 %reduce_sum.9 = f32[1024]{0:T(1024)S(1)} reduce(f32[512,1024]{1,0:T(8,128)} %param.6, f32[]{:T(128)} %constant.5.clone.1), dimensions={0}, to_apply=%region_0.0 | reduce | flops 523264 | bytes 2101252 | tf_op jit(solution)/shard_map/reduce_sum | solution.py:11
  8.4 40.5 %psum.7 = f32[1024]{0:T(1024)S(1)} all-reduce(f32[1024]{0:T(1024)S(1)} %reduce_sum.9), channel_id=1, replica_groups=mesh['row'=8,'col'=4] {'row','col'}, use_global_device_ids=true, to_apply=%region_1.0 | all-reduce | flops 1024 | bytes 8192 | tf_op jit(solution)/shard_map/psum | solution.py:11
  49.0 0.7 fusion
  49.7 0.1 dynamic_slice.3
  49.8 1.8 %multiply_convert_fusion = bf16[128,1024]{1,0:T(8,128)(2,1)} fusion(f32[128,1024]{1,0:T(8,128)} %param.5, f32[128]{0:T(128)S(1)} %dynamic_slice.3, f32[1024]{0:T(1024)S(1)} %get-tuple-element.6, f32[1024]{0:T(1024)S(1)} %get-tuple-element.5), kind=kLoop, calls=%fused_computation.2 | loop fusion | flops 524288 | bytes 795136 | tf_op jit(solution)/shard_map/convert_element_type | solution.py:19
  51.6 0.0 all-gather.5.cloned.1.call-update
  51.7 0.0 all-gather.3.cloned.1.call-start
  51.7 0.0 copy-done
  51.7 1.3 divide_convert_fusion
  53.0 0.0 all-gather.3.cloned.1.call-update
  53.0 0.0 copy-done.1
  53.0 0.1 copy.6
  53.1 5.5 %mul.37 = f32[4,512,2,512]{3,2,1,0:T(2,128)} broadcast(f32[4,2]{1,0:T(4,128)S(1)} %copy.6), dimensions={0,2} | broadcast | bytes 8388640 | tf_op jit(solution)/shard_map/mul | solution.py:30
  58.6 8.9 %copy.8 = f32[256,8,2,512]{3,1,2,0:T(8,128)} copy(f32[256,8,2,512]{3,2,1,0:T(2,128)} %bitcast.8) | data formatting | bytes 16777216
  67.5 32.1 %all-gather.5.cloned.1.call-done = bf16[1024,1024]{1,0:T(8,128)(2,1)} async-done(((bf16[128,1024]{1,0:T(8,128)(2,1)}), bf16[1024,1024]{1,0:T(8,128)(2,1)}) %all-gather.5.cloned.1.call-update) | async-done | bytes 2097168 | tf_op jit(solution)/shard_map/all_gather | solution.py:20
  99.6 36.9 %all-gather.3.cloned.1.call-done = bf16[2048,1024]{1,0:T(8,128)(2,1)} async-done(((bf16[512,1024]{1,0:T(8,128)(2,1)}), bf16[2048,1024]{1,0:T(8,128)(2,1)}) %all-gather.3.cloned.1.call-update) | async-done | bytes 4194320 | tf_op jit(solution)/shard_map/all_gather | solution.py:23
  136.5 13.5 %add_convert_fusion = bf16[2048,1024]{1,0:T(8,128)(2,1)} fusion(f32[2048,1024]{1,0:T(8,128)} %bitcast.9, bf16[2048,1024]{1,0:T(8,128)(2,1)} %param.7, bf16[2048,1024]{1,0:T(8,128)(2,1)} %all-gather.3.cloned.1.call-done, bf16[1024,1024]{1,0:T(8,128)(2,1)} %all-gather.5.cloned.1.call-done), kind=kOutput, calls=%fused_computation | convolution fusion | flops 4305453056 | bytes 23068672 | tf_op jit(solution)/shard_map/dot_general | solution.py:22
  (3 shorter events, 0.0 us)
Async XLA Ops:
  6.5 45.2 %copy-start = (f32[512,1024]{1,0:T(8,128)S(1)}, f32[512,1024]{1,0:T(8,128)}, u32[]{:S(2)}) copy-start(f32[512,1024]{1,0:T(8,128)} %param.6) | copy-start | bytes 6291460
  6.5 46.5 %copy-start.1 = (s32[4,2]{0,1:T(2,128)S(1)}, s32[4,2]{0,1:T(2,128)}, u32[]{:S(2)}) copy-start(s32[4,2]{0,1:T(2,128)} %param.9) | copy-start | bytes 100
  6.5 93.1 %all-gather.5.cloned.1.call-start = ((), (), s32[]{:S(2)}) async-start(), calls=%async_computation.1 | async-start | bytes 2359296 | tf_op jit(solution)/shard_map/all_gather | solution.py:20
  51.7 84.8 %all-gather.3.cloned.1.call-start = ((), (), s32[]{:S(2)}) async-start(), calls=%async_computation | async-start | bytes 5242880 | tf_op jit(solution)/shard_map/all_gather | solution.py:23
Sparse Core Ops, SparseCore 0:
  51.8 47.7 all-gather.4
  101.2 35.2 all-gather.2
where the time goes:
time: 157 us
  waiting for transfers between devices  69 us (44%)
  blocking collectives  40.5 us (26%)
  local copies, waits for them, and re-layouts  14.6 us (9%)
  matrix products  13.5 us (9%)
  between operations  13.4 us (9%)
  other arithmetic  5.75 us (4%)
    psum x1, blocking collectives, on_device(): totals = lax.psum(jnp.sum(old_dosage, axis=0), ('row', 'col'))  40.5 us
    all_gather x1, waiting for transfers between devices, on_device(): lax.all_gather(old_mine, 'col', axis=0, tiled=True)  36.9 us
    all_gather x1, waiting for transfers between devices, on_device(): new_scores = lax.all_gather(scores_mine, 'row', axis=0, tiled=True)  32.1 us
    dot_general x1, matrix products, on_device(): lax.dot_general(lax.all_gather(old_mine, 'col', axis=0, tiled=True), new_...  13.5 us
    unnamed x6, local copies, waits for them, and re-layouts  8.95 us
    mul x1, local copies, waits for them, and re-layouts, on_device(): masked_update = scaled * affected.astype(jnp.float32)[:, None, :, None]  5.45 us
  transfers between devices with their start and end apart: 2, of which 2 were waited for; matrix products, arithmetic and copies ran while one was open for 10% of the time, Pallas kernels for 0%

commit v1 on v0

v1 whole, which is shorter than its diff:
```python
import functools

import jax
import jax.numpy as jnp
from jax import lax
from jax.experimental import pallas as pl
from jax.experimental.pallas import tpu as pltpu
from jax.sharding import PartitionSpec as P

MESH = pl.DeviceIdType.MESH
CORES = 2
OLD_CHUNKS = 4
NEW_CHUNKS = 2
FOLD = 128


def kernel(
    n_row, n_col, new_hbm, old_hbm, grm_hbm, counts_ref, affected_ref, out_ref,
    new_in, old_in, grm_in, new_buf, old_buf, part, part_row,
    load_sem, col_send, col_recv, row_send, row_recv,
    x_send, sib_send, old_recv, right_send, left_send, y_send, new_recv,
):
    snps = new_in.shape[1]
    new_rows, old_rows = new_in.shape[0], old_in.shape[0]
    out_rows, out_cols = out_ref.shape
    tile = out_cols // counts_ref.shape[0]
    minor = 1 << ((n_row.bit_length() - 1) // 2)
    major = n_row // minor
    chips = n_col // CORES
    old_chunk, new_chunk = old_rows // OLD_CHUNKS, new_rows // NEW_CHUNKS
    group = minor * new_rows
    folds = snps // FOLD

    row, col = lax.axis_index("row"), lax.axis_index("col")
    a, b = row // minor, row % minor
    chip, core = col // CORES, col % CORES
    sibling = chip * CORES + (CORES - 1 - core)

    old_load = pltpu.make_async_copy(old_hbm, old_in, load_sem.at[0])
    new_load = pltpu.make_async_copy(new_hbm, new_in, load_sem.at[1])
    grm_load = pltpu.make_async_copy(grm_hbm, grm_in, load_sem.at[2])
    old_load.start()
    new_load.start()

    barrier = pltpu.get_barrier_semaphore()
    for d in range(1, n_col):
        pl.semaphore_signal(barrier, inc=1, device_id=(row, (col + d) % n_col), device_id_type=MESH)
    for d in range(1, n_row):
        pl.semaphore_signal(barrier, inc=1, device_id=((row + d) % n_row, col), device_id_type=MESH)

    old_load.wait()
    grm_load.start()
    mine = jnp.sum(old_in[...], axis=0, keepdims=True)
    for f in range(folds):
        part[pl.ds(col, 1), f, :] = mine[:, f * FOLD:(f + 1) * FOLD]
    pl.semaphore_wait(barrier, n_col - 1 + n_row - 1)

    def exchange(buf, me, count, send, recv, target):
        for d in range(1, count):
            pltpu.make_async_remote_copy(
                buf.at[me], buf.at[me], send.at[d], recv.at[me],
                device_id=target((me + d) % count), device_id_type=MESH,
            ).start()
        for d in range(1, count):
            other = (me + d) % count
            pltpu.make_async_remote_copy(
                buf.at[other], buf.at[other], send.at[d], recv.at[other],
                device_id=target(other), device_id_type=MESH,
            ).wait()
        total = buf[0]
        for i in range(1, count):
            total = total + buf[i]
        return total

    col_total = exchange(part, col, n_col, col_send, col_recv, lambda i: (row, i))
    part_row[row] = col_total
    total = exchange(part_row, row, n_row, row_send, row_recv, lambda i: (i, col))
    totals = jnp.concatenate([total[f:f + 1] for f in range(folds)], axis=1)
    doubled = totals / (old_rows * n_row * n_col)
    inverse = 1.0 / jnp.sqrt(doubled * (1.0 - 0.5 * doubled) + 0.1)

    def ds(start, size, step):
        return pl.ds(pl.multiple_of(start, step), size)

    def old_part(j, k):
        return old_buf.at[ds(j * old_rows + k * old_chunk, old_chunk, old_chunk), :]

    def new_part(r, k):
        return new_buf.at[ds(r * new_rows + k * new_chunk, new_chunk, new_chunk), :]

    def old_copy(j, k, send, to):
        return pltpu.make_async_remote_copy(
            old_part(j, k), old_part(j, k), send, old_recv.at[j, k],
            device_id=(row, to), device_id_type=MESH,
        )

    def new_copy(r, k, send, to):
        return pltpu.make_async_remote_copy(
            new_part(r, k), new_part(r, k), send, new_recv.at[r, k],
            device_id=(to, col), device_id_type=MESH,
        )

    sends = []

    def start_if(cond, copy):
        @pl.when(cond)
        def _():
            copy.start()
        sends.append((cond, copy))

    def send_y(z, s, k):
        out = []
        for d in range(1, minor):
            out.append(new_copy(z * minor + b, k, y_send.at[s, d, k], a * minor + (b + d) % minor))
        return out

    new_load.wait()
    first = (row * new_rows) % tile
    count = counts_ref[(row * new_rows) // tile]
    for k in range(NEW_CHUNKS):
        place = lax.broadcasted_iota(jnp.int32, (new_chunk, 1), 0) + (first + k * new_chunk)
        usable = (place < count).astype(jnp.float32)
        rows = new_in[k * new_chunk:(k + 1) * new_chunk, :]
        new_buf[ds(row * new_rows + k * new_chunk, new_chunk, new_chunk), :] = (
            (rows - doubled) * inverse * usable
        ).astype(jnp.bfloat16)
        start_if(a < major - 1, new_copy(row, k, right_send.at[0, k], row + minor))
        start_if(a > 0, new_copy(row, k, left_send.at[0, k], row - minor))
        for copy in send_y(a, 0, k):
            copy.start()
            sends.append((None, copy))
    for k in range(OLD_CHUNKS):
        rows = old_in[k * old_chunk:(k + 1) * old_chunk, :]
        old_buf[ds(col * old_rows + k * old_chunk, old_chunk, old_chunk), :] = (
            (rows - doubled) * inverse
        ).astype(jnp.bfloat16)
        for d in range(1, chips):
            copy = old_copy(col, k, x_send.at[d, k], (chip + d) % chips * CORES + core)
            copy.start()
            sends.append((None, copy))
        copy = old_copy(col, k, sib_send.at[0, k], sibling)
        copy.start()
        sends.append((None, copy))

    grm_load.wait()

    def relay(s):
        for k in range(NEW_CHUNKS):
            for left in (True, False):
                z = a - 1 - s if left else a + 1 + s
                valid = z >= 0 if left else z < major
                onward = valid & (a < major - 1) if left else valid & (a > 0)
                r = z * minor + b
                dest = row + minor if left else row - minor
                send = right_send if left else left_send

                @pl.when(valid)
                def _():
                    new_copy(r, k, send.at[s + 1, k], row).wait_recv()
                start_if(onward, new_copy(r, k, send.at[s + 1, k], dest))
                slot = 1 + 2 * s + (0 if left else 1)
                for copy in send_y(z, slot, k):
                    start_if(valid, copy)

    def wait_y(z):
        for k in range(NEW_CHUNKS):
            for d in range(1, minor):
                r = z * minor + (b + d) % minor
                new_copy(r, k, y_send.at[0, d, k], row).wait_recv()

    def forward_old(k):
        for d in range(1, chips):
            j = (chip + d) % chips * CORES + core
            old_copy(j, k, sib_send.at[d, k], sibling).wait_recv()
            copy = old_copy(j, k, sib_send.at[d, k], sibling)
            copy.start()
            sends.append((None, copy))

    def wait_sib_own():
        for k in range(OLD_CHUNKS):
            old_copy(sibling, k, sib_send.at[0, k], sibling).wait_recv()

    def wait_sib_forwarded(k):
        for d in range(1, chips):
            j = (chip + d) % chips * CORES + (CORES - 1 - core)
            old_copy(j, k, sib_send.at[d, k], sibling).wait_recv()

    def block(z, start, size):
        cols = ds(z * group, group, group)
        rows = ds(start, size, size)
        mark = affected_ref[start // tile, (z * group) // tile].astype(jnp.float32)
        product = lax.dot_general(
            old_buf[rows, :], new_buf[cols, :], (((1,), (1,)), ((), ())),
            preferred_element_type=jnp.float32,
        )
        out_ref[rows, cols] = (
            grm_in[rows, cols].astype(jnp.float32) + product * (mark / snps)
        ).astype(jnp.bfloat16)

    def local_rows(z):
        size = min(256, old_rows)
        per = old_rows // size

        @pl.loop(0, CORES * per)
        def _(i):
            block(z, chip * CORES * old_rows + i * size, size)

    def far_rows(z, k, which):
        for d in range(1, chips):
            for c in which:
                j = (chip + d) % chips * CORES + c
                block(z, j * old_rows + k * old_chunk, old_chunk)

    both = (core, CORES - 1 - core)

    def far_loop(z, k0, k1):
        @pl.loop(k0, k1)
        def _(k):
            far_rows(z, k, both)

    def step_groups(s, body):
        for left in (True, False):
            z = a - 1 - s if left else a + 1 + s

            @pl.when(z >= 0 if left else z < major)
            def _():
                body(z)

    relay(0)
    forward_old(0)
    wait_sib_own()
    wait_y(a)
    local_rows(a)
    for s in range(1, major - 1):
        relay(s)
        if s < OLD_CHUNKS - 1:
            forward_old(s)
    for k in range(major - 1, OLD_CHUNKS - 1):
        forward_old(k)
    for k in range(OLD_CHUNKS - 1):
        wait_sib_forwarded(k)
    far_loop(a, 0, OLD_CHUNKS - 1)
    last = OLD_CHUNKS - 1

    def most(z):
        wait_y(z)
        local_rows(z)
        far_loop(z, 0, last)

    for s in range(major - 2):
        step_groups(s, most)
    forward_old(last)

    step_groups(major - 2, most)
    wait_sib_forwarded(last)

    @pl.loop(0, major)
    def _(z):
        far_rows(z, last, both)

    for cond, copy in sends:
        if cond is None:
            copy.wait_send()
        else:
            @pl.when(cond)
            def _():
                copy.wait_send()


def on_device(new_dosage, old_dosage, grm, counts, affected):
    n_row, n_col = lax.axis_size("row"), lax.axis_size("col")
    new_rows, snps = new_dosage.shape
    old_rows = old_dosage.shape[0]
    minor = 1 << ((n_row.bit_length() - 1) // 2)
    major = n_row // minor
    chips = n_col // CORES
    dma = pltpu.SemaphoreType.DMA
    hbm = pl.BlockSpec(memory_space=pltpu.HBM)
    smem = pl.BlockSpec(memory_space=pltpu.SMEM)
    return pl.pallas_call(
        functools.partial(kernel, n_row, n_col),
        out_shape=jax.ShapeDtypeStruct(grm.shape, grm.dtype),
        in_specs=[hbm, hbm, hbm, smem, smem],
        out_specs=pl.BlockSpec(memory_space=pltpu.VMEM),
        scratch_shapes=[
            pltpu.VMEM((new_rows, snps), jnp.float32),
            pltpu.VMEM((old_rows, snps), jnp.float32),
            pltpu.VMEM(grm.shape, grm.dtype),
            pltpu.VMEM((new_rows * n_row, snps), jnp.bfloat16),
            pltpu.VMEM((old_rows * n_col, snps), jnp.bfloat16),
            pltpu.VMEM((n_col, snps // FOLD, FOLD), jnp.float32),
            pltpu.VMEM((n_row, snps // FOLD, FOLD), jnp.float32),
            dma((3,)),
            dma((n_col,)),
            dma((n_col,)),
            dma((n_row,)),
            dma((n_row,)),
            dma((chips, OLD_CHUNKS)),
            dma((chips, OLD_CHUNKS)),
            dma((n_col, OLD_CHUNKS)),
            dma((major, NEW_CHUNKS)),
            dma((major, NEW_CHUNKS)),
            dma((2 * major, minor, NEW_CHUNKS)),
            dma((n_row, NEW_CHUNKS)),
        ],
        compiler_params=pltpu.CompilerParams(
            collective_id=0, has_side_effects=True, vmem_limit_bytes=40 * 1024 * 1024
        ),
    )(new_dosage, old_dosage, grm, counts, affected)


def solution(mesh):
    return jax.shard_map(
        on_device,
        mesh=mesh,
        in_specs=(
            P(("col", "row"), None),
            P(("row", "col"), None),
            P("row", "col"),
            P("col"),
            P("row", "col"),
        ),
        out_specs=P("row", "col"),
        check_vma=False,
    )
```

time: 157 us -> 54.7 us (0.35)
  waiting for transfers between devices: 69 us -> 0 us
  Pallas kernels: 0 us -> 46.2 us
  blocking collectives: 40.5 us -> 0 us
  matrix products: 13.5 us -> 0 us
  between operations: 13.4 us -> 0.01 us
  local copies, waits for them, and re-layouts: 14.6 us -> 8.25 us
  other arithmetic: 5.75 us -> 0 us
    all_gather x2 -> x0, waiting for transfers between devices: 69 us -> none  [the longest x1 36.9 us: on_device(): lax.all_gather(old_mine, 'col', axis=0, tiled=True)]
    pallas_call x0 -> x1, Pallas kernels: none -> 46.2 us  [on_device(): pl.pallas_call(functools.partial(kernel, n_row, n_col), out_shape=jax.Sha...]
    psum x1 -> x0, blocking collectives: 40.5 us -> none  [on_device(): totals = lax.psum(jnp.sum(old_dosage, axis=0), ('row', 'col'))]
    dot_general x1 -> x0, matrix products: 13.5 us -> none  [on_device(): lax.dot_general(lax.all_gather(old_mine, 'col', axis=0, tiled=True), new_...]
    mul x1 -> x0, local copies, waits for them, and re-layouts: 5.45 us -> none  [on_device(): masked_update = scaled * affected.astype(jnp.float32)[:, None, :, None]]
    convert_element_type x3 -> x0, other arithmetic: 3.12 us -> none  [the longest x1 1.84 us: on_device(): ((new_dosage - doubled) / spread * usable_mine[:, None]).astype(jnp.bfloa...]
    reduce_sum x1 -> x0, other arithmetic: 1.89 us -> none  [on_device(): totals = lax.psum(jnp.sum(old_dosage, axis=0), ('row', 'col'))]
    unnamed x6 -> x10, local copies, waits for them, and re-layouts: 8.95 us -> 8.25 us
  transfers between devices with their start and end apart: 2 -> 0, of which waited for: 2 -> 0; matrix products, arithmetic and copies ran while one was open for 10% -> 0% of each run, Pallas kernels for 0% -> 0%
where the time goes in v1:
time: 54.7 us; the launch traced here: 54.5 us
  Pallas kernels  46.2 us (84%)
  local copies, waits for them, and re-layouts  8.25 us (15%)
    pallas_call x1, Pallas kernels, on_device(): pl.pallas_call(functools.partial(kernel, n_row, n_col), out_shape=jax.Sha...  46.2 us
    unnamed x10, local copies, waits for them, and re-layouts  8.25 us

profile of v1, /device:TPU:1, one launch (start us, length us, event | category | flops | bytes accessed | tf_op | source)
XLA Modules:
  0.0 54.5 jit_solution(7196027269356254892)
XLA Ops:
  0.0 0.8 %copy.6.affected_ref = s32[4,2]{1,0:T(4,128)S(1)} copy(s32[4,2]{0,1:T(2,128)} %param.9) | data formatting | bytes 64 | tf_op args[4]
  0.8 0.0 copy-start
  0.8 2.2 %copy-done = bf16[2048,1024]{1,0:T(8,128)(2,1)S(1)} copy-done((bf16[2048,1024]{1,0:T(8,128)(2,1)S(1)}, bf16[2048,1024]{1,0:T(8,128)(2,1)}, u32[]{:S(2)}) %copy-start) | copy-done | bytes 4194328
  3.0 0.0 copy-start.1
  3.0 1.6 %copy-done.1 = f32[512,1024]{1,0:T(8,128)S(1)} copy-done((f32[512,1024]{1,0:T(8,128)S(1)}, f32[512,1024]{1,0:T(8,128)}, u32[]{:S(2)}) %copy-start.1) | copy-done | bytes 2097176
  4.5 0.0 copy-start.2
  4.5 1.0 %copy-done.2 = f32[128,1024]{1,0:T(8,128)S(1)} copy-done((f32[128,1024]{1,0:T(8,128)S(1)}, f32[128,1024]{1,0:T(8,128)}, u32[]{:S(2)}) %copy-start.2) | copy-done | bytes 524312
  5.6 0.0 copy-start.3
  5.6 0.7 %copy-done.3 = s32[2]{0:T(128)S(1)} copy-done((s32[2]{0:T(128)S(1)}, s32[2]{0:T(128)}, u32[]{:S(2)}) %copy-start.3) | copy-done | bytes 32
  6.2 46.2 %shard_map.55 = bf16[2048,1024]{1,0:T(8,128)(2,1)S(1)} custom-call(f32[128,1024]{1,0:T(8,128)S(1)} %copy-done.2, f32[512,1024]{1,0:T(8,128)S(1)} %copy-done.1, bf16[2048,1024]{1,0:T(8,128)(2,1)S(1)} %copy-done, s32[2]{0:T(128)S(1)} %copy-done.3, s32[4,2]{1,0:T(4,128)S(1)} %copy.6.affected_ref), custom_call_target="tpu_custom_call" | custom-call | tf_op jit(solution)/shard_map/pallas_call | solution.py:280
  52.5 2.0 %copy.8 = bf16[2048,1024]{1,0:T(8,128)(2,1)} copy(bf16[2048,1024]{1,0:T(8,128)(2,1)S(1)} %shard_map.55) | data formatting | bytes 8388608
Async XLA Ops:
  0.8 2.2 %copy-start = (bf16[2048,1024]{1,0:T(8,128)(2,1)S(1)}, bf16[2048,1024]{1,0:T(8,128)(2,1)}, u32[]{:S(2)}) copy-start(bf16[2048,1024]{1,0:T(8,128)(2,1)} %grm_hbm.1) | copy-start | bytes 12582916
  3.0 1.6 %copy-start.1 = (f32[512,1024]{1,0:T(8,128)S(1)}, f32[512,1024]{1,0:T(8,128)}, u32[]{:S(2)}) copy-start(f32[512,1024]{1,0:T(8,128)} %old_hbm.1) | copy-start | bytes 6291460
  4.5 1.0 %copy-start.2 = (f32[128,1024]{1,0:T(8,128)S(1)}, f32[128,1024]{1,0:T(8,128)}, u32[]{:S(2)}) copy-start(f32[128,1024]{1,0:T(8,128)} %new_hbm.1) | copy-start | bytes 1572868
  5.6 0.7 %copy-start.3 = (s32[2]{0:T(128)S(1)}, s32[2]{0:T(128)}, u32[]{:S(2)}) copy-start(s32[2]{0:T(128)} %counts_ref.1) | copy-start | bytes 28

commit v2 on v1

--- a/solution.py
+++ b/solution.py
@@ -11,12 +11,15 @@
 CORES = 2
 OLD_CHUNKS = 4
 NEW_CHUNKS = 2
+CODED = 2
 FOLD = 128
+LEVELS = 32767
+STRIP = 32
 
 
 def kernel(
     n_row, n_col, new_hbm, old_hbm, grm_hbm, counts_ref, affected_ref, out_ref,
-    new_in, old_in, grm_in, new_buf, old_buf, part, part_row,
+    new_in, old_in, grm_in, new_code, old_code, new_buf, old_buf, part, part_row,
     load_sem, col_send, col_recv, row_send, row_recv,
     x_send, sib_send, old_recv, right_send, left_send, y_send, new_recv,
 ):
@@ -53,14 +56,82 @@
     mine = jnp.sum(old_in[...], axis=0, keepdims=True)
     for f in range(folds):
         part[pl.ds(col, 1), f, :] = mine[:, f * FOLD:(f + 1) * FOLD]
-    pl.semaphore_wait(barrier, n_col - 1 + n_row - 1)
-
-    def exchange(buf, me, count, send, recv, target):
+    def ds(start, size, step):
+        return pl.ds(pl.multiple_of(start, step), size)
+
+    coded_rows = CODED * old_chunk
+
+    def old_part(j, k):
+        if k < CODED:
+            return old_code.at[ds(j * coded_rows + k * old_chunk, old_chunk, old_chunk), :]
+        return exact_part(j, k)
+
+    def exact_part(j, k):
+        return old_buf.at[ds(j * old_rows + k * old_chunk, old_chunk, old_chunk), :]
+
+    def new_part(r, k):
+        return new_code.at[ds(r * new_rows + k * new_chunk, new_chunk, new_chunk), :]
+
+    def old_copy(j, k, send, to):
+        return pltpu.make_async_remote_copy(
+            old_part(j, k), old_part(j, k), send, old_recv.at[j, k],
+            device_id=(row, to), device_id_type=MESH,
+        )
+
+    def own_copy(j, k):
+        return pltpu.make_async_remote_copy(
+            exact_part(j, k), exact_part(j, k), sib_send.at[0, k], old_recv.at[j, k],
+            device_id=(row, sibling), device_id_type=MESH,
+        )
+
+    def new_copy(r, k, send, to):
+        return pltpu.make_async_remote_copy(
+            new_part(r, k), new_part(r, k), send, new_recv.at[r, k],
+            device_id=(to, col), device_id_type=MESH,
+        )
+
+    sends = []
+
+    def start(copy, cond=None):
+        if cond is None:
+            copy.start()
+        else:
+            @pl.when(cond)
+            def _():
+                copy.start()
+        sends.append((cond, copy))
+
+    def send_y(z, s, k):
+        return [
+            new_copy(z * minor + b, k, y_send.at[s, d, k], a * minor + (b + d) % minor)
+            for d in range(1, minor)
+        ]
+
+    def encode(x):
+        return ((x * LEVELS + 0.5).astype(jnp.int32) - LEVELS).astype(jnp.int16)
+
+    new_load.wait()
+    new_code[ds(row * new_rows, new_rows, new_rows), :] = encode(new_in[...])
+    old_code[ds(col * coded_rows, coded_rows, coded_rows), :] = encode(old_in[:coded_rows, :])
+
+    def send_new(k):
+        start(new_copy(row, k, right_send.at[0, k], row + minor), a < major - 1)
+        start(new_copy(row, k, left_send.at[0, k], row - minor), a > 0)
+        for copy in send_y(a, 0, k):
+            start(copy)
+
+    def send_old(k):
+        for d in range(1, chips):
+            start(old_copy(col, k, x_send.at[d, k], (chip + d) % chips * CORES + core))
+
+    def send_sums(buf, me, count, send, recv, target):
         for d in range(1, count):
             pltpu.make_async_remote_copy(
                 buf.at[me], buf.at[me], send.at[d], recv.at[me],
                 device_id=target((me + d) % count), device_id_type=MESH,
             ).start()
+
+    def take_sums(buf, me, count, send, recv, target):
         for d in range(1, count):
             other = (me + d) % count
             pltpu.make_async_remote_copy(
@@ -72,77 +143,18 @@
             total = total + buf[i]
         return total
 
-    col_total = exchange(part, col, n_col, col_send, col_recv, lambda i: (row, i))
-    part_row[row] = col_total
-    total = exchange(part_row, row, n_row, row_send, row_recv, lambda i: (i, col))
-    totals = jnp.concatenate([total[f:f + 1] for f in range(folds)], axis=1)
-    doubled = totals / (old_rows * n_row * n_col)
-    inverse = 1.0 / jnp.sqrt(doubled * (1.0 - 0.5 * doubled) + 0.1)
-
-    def ds(start, size, step):
-        return pl.ds(pl.multiple_of(start, step), size)
-
-    def old_part(j, k):
-        return old_buf.at[ds(j * old_rows + k * old_chunk, old_chunk, old_chunk), :]
-
-    def new_part(r, k):
-        return new_buf.at[ds(r * new_rows + k * new_chunk, new_chunk, new_chunk), :]
-
-    def old_copy(j, k, send, to):
-        return pltpu.make_async_remote_copy(
-            old_part(j, k), old_part(j, k), send, old_recv.at[j, k],
-            device_id=(row, to), device_id_type=MESH,
-        )
-
-    def new_copy(r, k, send, to):
-        return pltpu.make_async_remote_copy(
-            new_part(r, k), new_part(r, k), send, new_recv.at[r, k],
-            device_id=(to, col), device_id_type=MESH,
-        )
-
-    sends = []
-
-    def start_if(cond, copy):
-        @pl.when(cond)
-        def _():
-            copy.start()
-        sends.append((cond, copy))
-
-    def send_y(z, s, k):
-        out = []
-        for d in range(1, minor):
-            out.append(new_copy(z * minor + b, k, y_send.at[s, d, k], a * minor + (b + d) % minor))
-        return out
-
-    new_load.wait()
-    first = (row * new_rows) % tile
-    count = counts_ref[(row * new_rows) // tile]
-    for k in range(NEW_CHUNKS):
-        place = lax.broadcasted_iota(jnp.int32, (new_chunk, 1), 0) + (first + k * new_chunk)
-        usable = (place < count).astype(jnp.float32)
-        rows = new_in[k * new_chunk:(k + 1) * new_chunk, :]
-        new_buf[ds(row * new_rows + k * new_chunk, new_chunk, new_chunk), :] = (
-            (rows - doubled) * inverse * usable
-        ).astype(jnp.bfloat16)
-        start_if(a < major - 1, new_copy(row, k, right_send.at[0, k], row + minor))
-        start_if(a > 0, new_copy(row, k, left_send.at[0, k], row - minor))
-        for copy in send_y(a, 0, k):
-            copy.start()
-            sends.append((None, copy))
-    for k in range(OLD_CHUNKS):
-        rows = old_in[k * old_chunk:(k + 1) * old_chunk, :]
-        old_buf[ds(col * old_rows + k * old_chunk, old_chunk, old_chunk), :] = (
-            (rows - doubled) * inverse
-        ).astype(jnp.bfloat16)
-        for d in range(1, chips):
-            copy = old_copy(col, k, x_send.at[d, k], (chip + d) % chips * CORES + core)
-            copy.start()
-            sends.append((None, copy))
-        copy = old_copy(col, k, sib_send.at[0, k], sibling)
-        copy.start()
-        sends.append((None, copy))
-
-    grm_load.wait()
+    over_col = (part, col, n_col, col_send, col_recv, lambda i: (row, i))
+    over_row = (part_row, row, n_row, row_send, row_recv, lambda i: (i, col))
+
+    pl.semaphore_wait(barrier, n_col - 1 + n_row - 1)
+    send_sums(*over_col)
+    send_new(0)
+    for k in range(CODED):
+        send_old(k)
+    part_row[row] = take_sums(*over_col)
+    send_sums(*over_row)
+    for k in range(1, NEW_CHUNKS):
+        send_new(k)
 
     def relay(s):
         for k in range(NEW_CHUNKS):
@@ -157,10 +169,10 @@
                 @pl.when(valid)
                 def _():
                     new_copy(r, k, send.at[s + 1, k], row).wait_recv()
-                start_if(onward, new_copy(r, k, send.at[s + 1, k], dest))
+                start(new_copy(r, k, send.at[s + 1, k], dest), onward)
                 slot = 1 + 2 * s + (0 if left else 1)
                 for copy in send_y(z, slot, k):
-                    start_if(valid, copy)
+                    start(copy, valid)
 
     def wait_y(z):
         for k in range(NEW_CHUNKS):
@@ -172,23 +184,21 @@
         for d in range(1, chips):
             j = (chip + d) % chips * CORES + core
             old_copy(j, k, sib_send.at[d, k], sibling).wait_recv()
-            copy = old_copy(j, k, sib_send.at[d, k], sibling)
-            copy.start()
-            sends.append((None, copy))
+            start(old_copy(j, k, sib_send.at[d, k], sibling))
 
     def wait_sib_own():
         for k in range(OLD_CHUNKS):
-            old_copy(sibling, k, sib_send.at[0, k], sibling).wait_recv()
+            own_copy(sibling, k).wait_recv()
 
     def wait_sib_forwarded(k):
         for d in range(1, chips):
             j = (chip + d) % chips * CORES + (CORES - 1 - core)
             old_copy(j, k, sib_send.at[d, k], sibling).wait_recv()
 
-    def block(z, start, size):
+    def block(z, first, size):
         cols = ds(z * group, group, group)
-        rows = ds(start, size, size)
-        mark = affected_ref[start // tile, (z * group) // tile].astype(jnp.float32)
+        rows = ds(first, size, size)
+        mark = affected_ref[(z * group) // tile, first // tile].astype(jnp.float32)
         product = lax.dot_general(
             old_buf[rows, :], new_buf[cols, :], (((1,), (1,)), ((), ())),
             preferred_element_type=jnp.float32,
@@ -227,9 +237,56 @@
                 body(z)
 
     relay(0)
+    total = take_sums(*over_row)
+    totals = jnp.concatenate([total[f:f + 1] for f in range(folds)], axis=1)
+    doubled = totals / (old_rows * n_row * n_col)
+    inverse = 1.0 / jnp.sqrt(doubled * (1.0 - 0.5 * doubled) + 0.1)
+    code_scale = inverse / LEVELS
+    code_shift = (1.0 - doubled) * inverse
+
+    for k in reversed(range(OLD_CHUNKS)):
+        rows = old_in[k * old_chunk:(k + 1) * old_chunk, :]
+        old_buf[ds(col * old_rows + k * old_chunk, old_chunk, old_chunk), :] = (
+            (rows - doubled) * inverse
+        ).astype(jnp.bfloat16)
+    for k in range(CODED, OLD_CHUNKS):
+        send_old(k)
+    for k in range(OLD_CHUNKS):
+        start(own_copy(col, k))
+    grm_load.wait()
+
+    def decode(codes):
+        return codes.astype(jnp.int32).astype(jnp.float32) * code_scale + code_shift
+
+    def decode_new(z):
+        count = counts_ref[(z * group) // tile]
+
+        @pl.loop(0, group // STRIP)
+        def _(i):
+            at = z * group + i * STRIP
+            place = lax.broadcasted_iota(jnp.int32, (STRIP, 1), 0) + at % tile
+            usable = (place < count).astype(jnp.float32)
+            rows = ds(at, STRIP, STRIP)
+            new_buf[rows, :] = (decode(new_code[rows, :]) * usable).astype(jnp.bfloat16)
+
+    def decode_old(k):
+        if k >= CODED:
+            return
+        for d in range(1, chips):
+            for c in both:
+                j = (chip + d) % chips * CORES + c
+
+                @pl.loop(0, old_chunk // STRIP)
+                def _(i):
+                    codes = old_code[ds(j * coded_rows + k * old_chunk + i * STRIP, STRIP, STRIP), :]
+                    old_buf[ds(j * old_rows + k * old_chunk + i * STRIP, STRIP, STRIP), :] = (
+                        decode(codes).astype(jnp.bfloat16)
+                    )
+
     forward_old(0)
+    wait_y(a)
+    decode_new(a)
     wait_sib_own()
-    wait_y(a)
     local_rows(a)
     for s in range(1, major - 1):
         relay(s)
@@ -239,11 +296,13 @@
         forward_old(k)
     for k in range(OLD_CHUNKS - 1):
         wait_sib_forwarded(k)
+        decode_old(k)
     far_loop(a, 0, OLD_CHUNKS - 1)
     last = OLD_CHUNKS - 1
 
     def most(z):
         wait_y(z)
+        decode_new(z)
         local_rows(z)
         far_loop(z, 0, last)
 
@@ -286,6 +345,8 @@
             pltpu.VMEM((new_rows, snps), jnp.float32),
             pltpu.VMEM((old_rows, snps), jnp.float32),
             pltpu.VMEM(grm.shape, grm.dtype),
+            pltpu.VMEM((new_rows * n_row, snps), jnp.int16),
+            pltpu.VMEM((old_rows // OLD_CHUNKS * CODED * n_col, snps), jnp.int16),
             pltpu.VMEM((new_rows * n_row, snps), jnp.bfloat16),
             pltpu.VMEM((old_rows * n_col, snps), jnp.bfloat16),
             pltpu.VMEM((n_col, snps // FOLD, FOLD), jnp.float32),
@@ -306,7 +367,7 @@
         compiler_params=pltpu.CompilerParams(
             collective_id=0, has_side_effects=True, vmem_limit_bytes=40 * 1024 * 1024
         ),
-    )(new_dosage, old_dosage, grm, counts, affected)
+    )(new_dosage, old_dosage, grm, counts, affected.T)
 
 
 def solution(mesh):

time: 54.7 us -> 50.3 us (0.920)
  Pallas kernels: 46.2 us -> 41.8 us
    pallas_call x1, Pallas kernels: 46.2 us -> 41.8 us  [on_device(): pl.pallas_call(functools.partial(kernel, n_row, n_col), out_shape=jax.Sha...]
    unnamed x10 -> x11, local copies, waits for them, and re-layouts: 8.25 us -> 8.17 us
where the time goes in v2:
time: 50.3 us; the launch traced here: 50 us
  Pallas kernels  41.8 us (83%)
  local copies, waits for them, and re-layouts  8.17 us (16%)
    pallas_call x1, Pallas kernels, on_device(): pl.pallas_call(functools.partial(kernel, n_row, n_col), out_shape=jax.Sha...  41.8 us
    unnamed x11, local copies, waits for them, and re-layouts  8.17 us

profile of v2, /device:TPU:1, one launch (start us, length us, event | category | flops | bytes accessed | tf_op | source)
XLA Modules:
  0.0 50.0 jit_solution(7717255483357403398)
XLA Ops:
  0.0 0.0 copy-start
  0.0 2.2 %copy-done = bf16[2048,1024]{1,0:T(8,128)(2,1)S(1)} copy-done((bf16[2048,1024]{1,0:T(8,128)(2,1)S(1)}, bf16[2048,1024]{1,0:T(8,128)(2,1)}, u32[]{:S(2)}) %copy-start) | copy-done | bytes 4194328
  2.2 0.0 copy-start.1
  2.2 1.6 %copy-done.1 = f32[512,1024]{1,0:T(8,128)S(1)} copy-done((f32[512,1024]{1,0:T(8,128)S(1)}, f32[512,1024]{1,0:T(8,128)}, u32[]{:S(2)}) %copy-start.1) | copy-done | bytes 2097176
  3.8 0.0 copy-start.2
  3.8 1.0 %copy-done.2 = f32[128,1024]{1,0:T(8,128)S(1)} copy-done((f32[128,1024]{1,0:T(8,128)S(1)}, f32[128,1024]{1,0:T(8,128)}, u32[]{:S(2)}) %copy-start.2) | copy-done | bytes 524312
  4.8 0.0 copy-start.3
  4.8 0.7 %copy-done.3 = s32[4,2]{0,1:T(2,128)S(1)} copy-done((s32[4,2]{0,1:T(2,128)S(1)}, s32[4,2]{0,1:T(2,128)}, u32[]{:S(2)}) %copy-start.3) | copy-done | bytes 56
  5.5 0.0 copy-start.4
  5.5 0.7 %copy-done.4 = s32[2]{0:T(128)S(1)} copy-done((s32[2]{0:T(128)S(1)}, s32[2]{0:T(128)}, u32[]{:S(2)}) %copy-start.4) | copy-done | bytes 32
  6.2 41.8 %shard_map.55 = bf16[2048,1024]{1,0:T(8,128)(2,1)S(1)} custom-call(f32[128,1024]{1,0:T(8,128)S(1)} %copy-done.2, f32[512,1024]{1,0:T(8,128)S(1)} %copy-done.1, bf16[2048,1024]{1,0:T(8,128)(2,1)S(1)} %copy-done, s32[2]{0:T(128)S(1)} %copy-done.4, s32[2,4]{1,0:T(2,128)S(1)} %bitcast.1), custom_call_target="tpu_custom_call" | custom-call | tf_op jit(solution)/shard_map/pallas_call | solution.py:339
  47.9 2.0 %copy.7 = bf16[2048,1024]{1,0:T(8,128)(2,1)} copy(bf16[2048,1024]{1,0:T(8,128)(2,1)S(1)} %shard_map.55) | data formatting | bytes 8388608
Async XLA Ops:
  0.0 2.2 %copy-start = (bf16[2048,1024]{1,0:T(8,128)(2,1)S(1)}, bf16[2048,1024]{1,0:T(8,128)(2,1)}, u32[]{:S(2)}) copy-start(bf16[2048,1024]{1,0:T(8,128)(2,1)} %grm_hbm.1) | copy-start | bytes 12582916
  2.2 1.6 %copy-start.1 = (f32[512,1024]{1,0:T(8,128)S(1)}, f32[512,1024]{1,0:T(8,128)}, u32[]{:S(2)}) copy-start(f32[512,1024]{1,0:T(8,128)} %old_hbm.1) | copy-start | bytes 6291460
  3.8 1.0 %copy-start.2 = (f32[128,1024]{1,0:T(8,128)S(1)}, f32[128,1024]{1,0:T(8,128)}, u32[]{:S(2)}) copy-start(f32[128,1024]{1,0:T(8,128)} %new_hbm.1) | copy-start | bytes 1572868
  4.8 0.7 %copy-start.3 = (s32[4,2]{0,1:T(2,128)S(1)}, s32[4,2]{0,1:T(2,128)}, u32[]{:S(2)}) copy-start(s32[4,2]{0,1:T(2,128)} %param.9) | copy-start | bytes 100
  5.5 0.7 %copy-start.4 = (s32[2]{0:T(128)S(1)}, s32[2]{0:T(128)}, u32[]{:S(2)}) copy-start(s32[2]{0:T(128)} %counts_ref.1) | copy-start | bytes 28

commit v3 on v2

--- a/solution.py
+++ b/solution.py
@@ -12,6 +12,7 @@
 OLD_CHUNKS = 4
 NEW_CHUNKS = 2
 CODED = 2
+PAIR = 2
 FOLD = 128
 LEVELS = 32767
 STRIP = 32
@@ -59,15 +60,19 @@
     def ds(start, size, step):
         return pl.ds(pl.multiple_of(start, step), size)
 
-    coded_rows = CODED * old_chunk
+    def score_place(j, k):
+        return ((j // CORES * OLD_CHUNKS + k) * CORES + j % CORES) * old_chunk
+
+    def code_place(j, k):
+        return ((j // CORES * CODED + k) * CORES + j % CORES) * old_chunk
 
     def old_part(j, k):
         if k < CODED:
-            return old_code.at[ds(j * coded_rows + k * old_chunk, old_chunk, old_chunk), :]
+            return old_code.at[ds(code_place(j, k), old_chunk, old_chunk), :]
         return exact_part(j, k)
 
     def exact_part(j, k):
-        return old_buf.at[ds(j * old_rows + k * old_chunk, old_chunk, old_chunk), :]
+        return old_buf.at[ds(score_place(j, k), old_chunk, old_chunk), :]
 
     def new_part(r, k):
         return new_code.at[ds(r * new_rows + k * new_chunk, new_chunk, new_chunk), :]
@@ -112,7 +117,10 @@
 
     new_load.wait()
     new_code[ds(row * new_rows, new_rows, new_rows), :] = encode(new_in[...])
-    old_code[ds(col * coded_rows, coded_rows, coded_rows), :] = encode(old_in[:coded_rows, :])
+    for k in range(CODED):
+        old_code[ds(code_place(col, k), old_chunk, old_chunk), :] = encode(
+            old_in[k * old_chunk:(k + 1) * old_chunk, :]
+        )
 
     def send_new(k):
         start(new_copy(row, k, right_send.at[0, k], row + minor), a < major - 1)
@@ -195,38 +203,34 @@
             j = (chip + d) % chips * CORES + (CORES - 1 - core)
             old_copy(j, k, sib_send.at[d, k], sibling).wait_recv()
 
-    def block(z, first, size):
+    def block(z, where, k0, count):
         cols = ds(z * group, group, group)
-        rows = ds(first, size, size)
-        mark = affected_ref[(z * group) // tile, first // tile].astype(jnp.float32)
+        unit = CORES * old_chunk
         product = lax.dot_general(
-            old_buf[rows, :], new_buf[cols, :], (((1,), (1,)), ((), ())),
-            preferred_element_type=jnp.float32,
-        )
-        out_ref[rows, cols] = (
-            grm_in[rows, cols].astype(jnp.float32) + product * (mark / snps)
-        ).astype(jnp.bfloat16)
+            old_buf[ds((where * OLD_CHUNKS + k0) * unit, count * unit, unit), :], new_buf[cols, :],
+            (((1,), (1,)), ((), ())), preferred_element_type=jnp.float32,
+        )
+        for i in range(count):
+            for c in range(CORES):
+                first = (where * CORES + c) * old_rows + (k0 + i) * old_chunk
+                rows = ds(first, old_chunk, old_chunk)
+                mark = affected_ref[(z * group) // tile, first // tile].astype(jnp.float32)
+                at = (i * CORES + c) * old_chunk
+                out_ref[rows, cols] = (
+                    grm_in[rows, cols].astype(jnp.float32)
+                    + product[at:at + old_chunk, :] * (mark / snps)
+                ).astype(jnp.bfloat16)
 
     def local_rows(z):
-        size = min(256, old_rows)
-        per = old_rows // size
-
-        @pl.loop(0, CORES * per)
+        @pl.loop(0, OLD_CHUNKS // PAIR)
         def _(i):
-            block(z, chip * CORES * old_rows + i * size, size)
-
-    def far_rows(z, k, which):
-        for d in range(1, chips):
-            for c in which:
-                j = (chip + d) % chips * CORES + c
-                block(z, j * old_rows + k * old_chunk, old_chunk)
+            block(z, chip, i * PAIR, PAIR)
+
+    def far_rows(z, k0, count):
+        for d in range(1, chips):
+            block(z, (chip + d) % chips, k0, count)
 
     both = (core, CORES - 1 - core)
-
-    def far_loop(z, k0, k1):
-        @pl.loop(k0, k1)
-        def _(k):
-            far_rows(z, k, both)
 
     def step_groups(s, body):
         for left in (True, False):
@@ -246,7 +250,7 @@
 
     for k in reversed(range(OLD_CHUNKS)):
         rows = old_in[k * old_chunk:(k + 1) * old_chunk, :]
-        old_buf[ds(col * old_rows + k * old_chunk, old_chunk, old_chunk), :] = (
+        old_buf[ds(score_place(col, k), old_chunk, old_chunk), :] = (
             (rows - doubled) * inverse
         ).astype(jnp.bfloat16)
     for k in range(CODED, OLD_CHUNKS):
@@ -278,8 +282,8 @@
 
                 @pl.loop(0, old_chunk // STRIP)
                 def _(i):
-                    codes = old_code[ds(j * coded_rows + k * old_chunk + i * STRIP, STRIP, STRIP), :]
-                    old_buf[ds(j * old_rows + k * old_chunk + i * STRIP, STRIP, STRIP), :] = (
+                    codes = old_code[ds(code_place(j, k) + i * STRIP, STRIP, STRIP), :]
+                    old_buf[ds(score_place(j, k) + i * STRIP, STRIP, STRIP), :] = (
                         decode(codes).astype(jnp.bfloat16)
                     )
 
@@ -297,14 +301,14 @@
     for k in range(OLD_CHUNKS - 1):
         wait_sib_forwarded(k)
         decode_old(k)
-    far_loop(a, 0, OLD_CHUNKS - 1)
+    far_rows(a, 0, OLD_CHUNKS - 1)
     last = OLD_CHUNKS - 1
 
     def most(z):
         wait_y(z)
         decode_new(z)
         local_rows(z)
-        far_loop(z, 0, last)
+        far_rows(z, 0, last)
 
     for s in range(major - 2):
         step_groups(s, most)
@@ -315,7 +319,7 @@
 
     @pl.loop(0, major)
     def _(z):
-        far_rows(z, last, both)
+        far_rows(z, last, 1)
 
     for cond, copy in sends:
         if cond is None:
@@ -338,7 +342,7 @@
     smem = pl.BlockSpec(memory_space=pltpu.SMEM)
     return pl.pallas_call(
         functools.partial(kernel, n_row, n_col),
-        out_shape=jax.ShapeDtypeStruct(grm.shape, grm.dtype),
+        out_shape=pltpu.VMEM(grm.shape, grm.dtype),
         in_specs=[hbm, hbm, hbm, smem, smem],
         out_specs=pl.BlockSpec(memory_space=pltpu.VMEM),
         scratch_shapes=[
@@ -365,7 +369,7 @@
             dma((n_row, NEW_CHUNKS)),
         ],
         compiler_params=pltpu.CompilerParams(
-            collective_id=0, has_side_effects=True, vmem_limit_bytes=40 * 1024 * 1024
+            collective_id=0, has_side_effects=True, vmem_limit_bytes=56 * 1024 * 1024
         ),
     )(new_dosage, old_dosage, grm, counts, affected.T)
 

time: 50.3 us -> 38.7 us (0.77)
  local copies, waits for them, and re-layouts: 8.17 us -> 2.02 us
  Pallas kernels: 41.8 us -> 36.5 us
    unnamed x11 -> x1, local copies, waits for them, and re-layouts: 8.17 us -> 2.02 us
    pallas_call x1, Pallas kernels: 41.8 us -> 36.5 us  [on_device(): pl.pallas_call(functools.partial(kernel, n_row, n_col), out_shape=pltpu.V...]
where the time goes in v3:
time: 38.7 us; the launch traced here: 38.5 us
  Pallas kernels  36.5 us (94%)
  local copies, waits for them, and re-layouts  2.02 us (5%)
    pallas_call x1, Pallas kernels, on_device(): pl.pallas_call(functools.partial(kernel, n_row, n_col), out_shape=pltpu.V...  36.5 us
    unnamed x1, local copies, waits for them, and re-layouts  2.02 us

profile of v3, /device:TPU:1, one launch (start us, length us, event | category | flops | bytes accessed | tf_op | source)
XLA Modules:
  0.0 38.5 jit_solution(530347760559102269)
XLA Ops:
  0.0 36.5 %shard_map.55 = bf16[2048,1024]{1,0:T(8,128)(2,1)S(1)} custom-call(f32[128,1024]{1,0:T(8,128)} %new_hbm.1, f32[512,1024]{1,0:T(8,128)} %old_hbm.1, bf16[2048,1024]{1,0:T(8,128)(2,1)} %grm_hbm.1, s32[2]{0:T(128)} %counts_ref.1, s32[2,4]{1,0:T(2,128)} %bitcast.1), custom_call_target="tpu_custom_call" | custom-call | tf_op jit(solution)/shard_map/pallas_call | solution.py:343
  36.5 2.0 %copy.7 = bf16[2048,1024]{1,0:T(8,128)(2,1)} copy(bf16[2048,1024]{1,0:T(8,128)(2,1)S(1)} %shard_map.55) | data formatting | bytes 8388608
